TPU v7x, 512 devices: a whole 4x4x16 slice. The times are simulated.
512 devices in a mesh: vocab: 128 (over z, y, core), width: 4 (over x).
Axes of the slice: x: 4, y: 4, z: 16, core: 2. Of those that a mesh axis runs over, the one named last changes fastest.
Arguments:
- qwen_hidden: bfloat16 [256, 8192], P('vocab', 'width'), may hold values from -96 to 96
- qwen_next_hidden: bfloat16 [256, 8192], P('vocab', 'width'), may hold values from -96 to 96
- llama_hidden: bfloat16 [256, 8192], P('vocab', 'width'), may hold values from -96 to 96
- llama_next_hidden: bfloat16 [256, 8192], P('vocab', 'width'), may hold values from -96 to 96
- qwen_head: bfloat16 [81920, 8192], P('vocab', 'width'), may hold values from -0.198873782 to 0.198873782
- llama_head: bfloat16 [65536, 8192], P('vocab', 'width'), may hold values from -0.198873782 to 0.198873782
- align_weights: bfloat16 [4, 128, 128], replicated, may hold values from 0 to 1, as said below
- qwen_links: int32 [1280, 3], replicated, may hold values from 0 to 1023, as said below
- llama_links: int32 [1024, 3], replicated, may hold values from 0 to 1023, as said below
- union_order: int32 [1024], replicated, may hold values from 0 to 1023, each once
- chosen: int32 [256], P('vocab'), may hold values from 0 to 131071
- model_weight: float32 [2], replicated, may hold values from 0.25 to 1
Outputs:
- next_logprob: float32 [256, 131072], P(None, ('vocab', 'width'))
- chosen_loglik: float32 [256], P('vocab')
Inputs may be any that keep to these rules, and one draw needn't show every extreme that they name: `qwen_links`: each row is (source block, union block, alignment matrix). Each of the 640 source blocks stands in exactly 2 rows; union blocks are below 1024; alignment matrices below 4. `llama_links`: each row is (source block, union block, alignment matrix). Each of the 512 source blocks stands in exactly 2 rows; every union block stands in exactly one row; alignment matrices below 4. `align_weights`: all entries positive; every row of every matrix sums to one up to bfloat16 rounding.
All inputs are finite; a program needn't handle non-finite values.
Results may differ from a plain program's by a relative error of at most 0.00075.
Values may be sent and summed in bfloat16 or wider, within the bound.
A program may use at most 64 MiB of HBM per device.

v0:
```python
import functools

import jax
import jax.numpy as jnp
from jax import lax
from jax.experimental import pallas as pl
from jax.experimental.pallas import tpu as pltpu
from jax.sharding import Mesh
from jax.sharding import PartitionSpec as P

BLOCK = 128
QB_DEV = 5
LB_DEV = 4
B_DEV = QB_DEV + LB_DEV
KINDS = 4
UBLOCKS = 1024
SMOOTHING = 0.01
UNIFORM = SMOOTHING / (UBLOCKS * BLOCK)
VOCAB = ("vocab_0", "vocab_1", "vocab_2")
PLANE = ("vocab_0", "vocab_1")
GROUP = ("vocab_1", "vocab_2")


def positions_of(union_order, blocks):
    places = jnp.arange(UBLOCKS, dtype=jnp.int32)
    return jnp.sum(jnp.where(union_order[None, :] == blocks[:, None], places[None, :], 0), axis=1)


def link_codes(links, union_order, blocks):
    codes = positions_of(union_order, links[:, 1]) * KINDS + links[:, 2]
    hit = links[:, 0][None, :] == jnp.arange(blocks, dtype=jnp.int32)[:, None]
    low = jnp.min(jnp.where(hit, codes[None, :], UBLOCKS * KINDS), axis=1)
    high = jnp.max(jnp.where(hit, codes[None, :], -1), axis=1)
    return low, high


def three_parts(value):
    first = lax.reduce_precision(value, 8, 7)
    rest = value - first
    second = lax.reduce_precision(rest, 8, 7)
    third = lax.reduce_precision(rest - second, 8, 7)
    return [part.astype(jnp.bfloat16) for part in (first, second, third)]


def chosen_codes(chosen):
    block = chosen // BLOCK
    codes = jnp.stack([block // 32, block % 32, chosen % BLOCK], axis=1)
    return jnp.pad(codes.astype(jnp.bfloat16), ((0, 0), (0, BLOCK - 3)))


def gathered_tiles(hidden_cat, chosen):
    rows, columns = hidden_cat.shape
    parts = hidden_cat.reshape(rows, 8, columns // 8).transpose(1, 0, 2)
    codes = jnp.broadcast_to(chosen_codes(chosen)[None], (8, rows, BLOCK))
    tile = lax.all_to_all(jnp.concatenate([parts, codes], axis=2), GROUP, 0, 0, tiled=True)
    tile = tile.reshape(8 * rows, -1)
    tiles = lax.all_gather(tile, "vocab_1")
    tiles = lax.all_gather(tiles, "vocab_0")
    return lax.all_gather(tiles, "vocab_2", axis=2)


def partial_logits(tiles, qwen_head, llama_head):
    chunk = tiles.shape[-1] - BLOCK
    found = []
    for tensor in range(4):
        head = qwen_head if tensor < 2 else llama_head
        total = 0.0
        for half in range(2):
            place = tensor * 2 + half
            rows = tiles[:, place // 2, place % 2, :, :chunk].reshape(-1, chunk)
            total = total + lax.dot_general(
                rows,
                head[:, half * chunk : (half + 1) * chunk],
                (((1,), (1,)), ((), ())),
                preferred_element_type=jnp.float32,
            )
        found.append(total)
    first = jnp.concatenate([found[0], found[2]], axis=1)
    second = jnp.concatenate([found[1], found[3]], axis=1)
    return jnp.stack([first, second])


def width_summed(partial):
    steps, rows, entries = partial.shape
    split = jnp.moveaxis(partial.reshape(steps, rows // 4, 4, entries), 2, 0)
    return jnp.sum(lax.all_to_all(split, "width", 0, 0, tiled=True), axis=0)


def row_message(logits, chosen_pos, chosen_col, own_low, own_high, align_weights):
    rows = logits.shape[1]
    q_cols = QB_DEV * BLOCK
    models = (slice(0, q_cols), slice(q_cols, B_DEV * BLOCK))
    one_hot = (chosen_col[:, None] == jnp.arange(BLOCK, dtype=jnp.int32)[None, :]).astype(jnp.bfloat16)
    columns = jnp.einsum("rj,kij->kri", one_hot, align_weights, preferred_element_type=jnp.float32)
    weight = jnp.zeros((rows, B_DEV, BLOCK), jnp.float32)
    for kind in range(KINDS):
        code = (chosen_pos * KINDS + kind)[:, None]
        count = (own_low[None, :] == code).astype(jnp.float32) + (own_high[None, :] == code).astype(jnp.float32)
        weight = weight + count[:, :, None] * columns[kind][:, None, :]
    weight = weight.reshape(rows, B_DEV * BLOCK)
    values, terms = [], []
    for cols in models:
        part = logits[0, :, cols]
        top = jnp.max(part, axis=1, keepdims=True)
        powers = jnp.exp(part - top)
        values += [top, jnp.sum(powers, 1, keepdims=True), jnp.sum(powers * weight[:, cols], 1, keepdims=True)]
    for cols in models:
        part = logits[1, :, cols]
        top = jnp.max(part, axis=1, keepdims=True)
        powers = jnp.exp(part - top)
        values += [top, jnp.sum(powers, 1, keepdims=True)]
        terms.append(powers.astype(jnp.bfloat16))
    parts = three_parts(jnp.concatenate(values, axis=1))
    blank = jnp.zeros((rows, BLOCK - 30), jnp.bfloat16)
    return jnp.concatenate([*terms, *parts, blank], axis=1)


def rescaled(tops, sums):
    factor = jnp.exp(tops - jnp.max(tops))
    return factor, jnp.sum(factor * sums)


def row_scales(message, model_weight):
    stats = message[:, B_DEV * BLOCK :].astype(jnp.float32)
    stats = stats[:, 0:10] + stats[:, 10:20] + stats[:, 20:30]
    prior = model_weight / (model_weight[0] + model_weight[1])
    masses = []
    for model in range(2):
        factor, total = rescaled(stats[:, 3 * model], stats[:, 3 * model + 1])
        value = 0.5 * jnp.sum(factor * stats[:, 3 * model + 2]) / total
        masses.append(prior[model] * ((1.0 - SMOOTHING) * value + UNIFORM))
    together = masses[0] + masses[1]
    scales = []
    for model in range(2):
        factor, total = rescaled(stats[:, 6 + 2 * model], stats[:, 7 + 2 * model])
        scales.append((masses[model] / together) * 0.5 * factor / total)
    return scales, jnp.log(together)


def map_kernel(low_ref, high_ref, terms_ref, weights_ref, out_ref):
    core = lax.axis_index("vocab_2")
    half = out_ref.shape[0]
    spot = lax.broadcasted_iota(jnp.int32, (half, BLOCK), 0)
    first = (16 * (spot // 4) + 8 * core + 2 * (spot % 4)) * KINDS
    for t in range(2):
        mixed = jnp.zeros((half, BLOCK), jnp.float32)
        for kind in range(KINDS):
            code = first + (t * KINDS + kind)
            total = jnp.zeros((half, BLOCK), jnp.float32)
            for b in range(B_DEV):
                hits = jnp.where(low_ref[b : b + 1, :] == code, 1.0, 0.0) + jnp.where(
                    high_ref[b : b + 1, :] == code, 1.0, 0.0
                )
                total += jnp.dot(
                    hits.astype(jnp.bfloat16),
                    terms_ref[:, b * BLOCK : (b + 1) * BLOCK],
                    preferred_element_type=jnp.float32,
                )
            mixed += jnp.dot(
                total.astype(jnp.bfloat16), weights_ref[kind], preferred_element_type=jnp.float32
            )
        out_ref[:, t * BLOCK : (t + 1) * BLOCK] = mixed.astype(out_ref.dtype)


def mapped(low, high, terms, align_weights):
    return pl.pallas_call(
        map_kernel,
        out_shape=jax.ShapeDtypeStruct((UBLOCKS // 4, 2 * BLOCK), jnp.bfloat16),
    )(low, high, terms, align_weights)


def by_source(codes, per_device):
    return codes.reshape(-1, 2, per_device).transpose(2, 1, 0).reshape(per_device, -1)


def local(
    qwen_hidden,
    qwen_next_hidden,
    llama_hidden,
    llama_next_hidden,
    qwen_head,
    llama_head,
    align_weights,
    qwen_links,
    llama_links,
    union_order,
    chosen,
    model_weight,
):
    core = lax.axis_index("vocab_2")
    width = lax.axis_index("width")
    owner = lax.axis_index(VOCAB)
    hidden_cat = jnp.concatenate(
        [qwen_hidden, qwen_next_hidden, llama_hidden, llama_next_hidden], axis=1
    )
    tiles = gathered_tiles(hidden_cat, chosen)
    codes = tiles[:, 0, 0, :, -BLOCK:][:, :, :3].astype(jnp.int32).reshape(-1, 4, 3)
    codes = lax.dynamic_index_in_dim(codes, width, 1, keepdims=False)
    chosen_pos = positions_of(union_order, codes[:, 0] * 32 + codes[:, 1])
    q_low, q_high = link_codes(qwen_links, union_order, qwen_links.shape[0] // 2)
    l_low, l_high = link_codes(llama_links, union_order, llama_links.shape[0] // 2)
    own_low, own_high = (
        jnp.concatenate(
            [
                lax.dynamic_slice(q, (owner * QB_DEV,), (QB_DEV,)),
                lax.dynamic_slice(l, (owner * LB_DEV,), (LB_DEV,)),
            ]
        )
        for q, l in ((q_low, l_low), (q_high, l_high))
    )
    low, high = (
        jnp.concatenate([by_source(q, QB_DEV), by_source(l, LB_DEV)])
        for q, l in ((q_low, l_low), (q_high, l_high))
    )
    logits = width_summed(partial_logits(tiles, qwen_head, llama_head))
    message = row_message(logits, chosen_pos, codes[:, 2], own_low, own_high, align_weights)
    message = lax.all_to_all(message, PLANE, 0, 0, tiled=True)
    message = lax.all_gather(message, "vocab_2", axis=0, tiled=True)
    (q_scale, l_scale), loglik = row_scales(message, model_weight)
    q_cols = QB_DEV * BLOCK
    terms = message[:, : B_DEV * BLOCK].astype(jnp.float32)
    terms = jnp.concatenate(
        [terms[:, :q_cols] * q_scale[:, None], terms[:, q_cols:] * l_scale[:, None]], axis=1
    ).astype(jnp.bfloat16)
    mixed = mapped(low, high, terms, align_weights)
    owned = lax.all_to_all(mixed, ("vocab_0", "vocab_1", "width"), 0, 0, tiled=True)
    next_logprob = jnp.log((1.0 - SMOOTHING) * owned.astype(jnp.float32) + UNIFORM)
    logliks = lax.all_gather(loglik, "width")
    return next_logprob, lax.dynamic_slice(logliks, (2 * core,), (2,))


def solution(mesh):
    torus = Mesh(
        mesh.devices.reshape(16, 4, 2, mesh.shape["width"]),
        ("vocab_0", "vocab_1", "vocab_2", "width"),
    )
    return jax.shard_map(
        local,
        mesh=torus,
        in_specs=(*[P(VOCAB, "width")] * 6, P(), P(), P(), P(), P(VOCAB), P()),
        out_specs=(P(None, (*VOCAB, "width")), P(VOCAB)),
        check_vma=False,
    )
```

profile of v0, /device:TPU:1, one launch (start us, length us, event | category | flops | bytes accessed | tf_op | source)
XLA Modules:
  0.0 270.9 jit_solution(17265054669885615857)
XLA Ops:
  8.9 13.9 %all_to_all.31 = bf16[8,2,1152]{2,1,0:T(2,128)(2,1)S(1)} all-to-all(bf16[8,2,1152]{2,1,0:T(2,128)(2,1)S(1)} %pad_maximum_fusion.3), channel_id=1, replica_groups=mesh['vocab_0'=16,'vocab_1'=4,'vocab_2'=2,'width'=4] {'vocab_1','vocab_2'}, dimensions={0} | all-to-all | bytes 73728 | tf_op jit(solution)/shard_map/all_to_all | solution.py:55
  22.9 9.9 %all_gather.24 = bf16[4,16,1152]{2,1,0:T(8,128)(2,1)} all-gather(bf16[1,16,1152]{2,1,0:T(8,128)(2,1)S(1)} %all_gather_reshape.3), channel_id=1, replica_groups=mesh['vocab_0'=16,'vocab_1'=4,'vocab_2'=2,'width'=4] {'vocab_1'}, dimensions={0}, use_global_device_ids=true | all-gather | bytes 184320 | tf_op jit(solution)/shard_map/all_gather | solution.py:57
  32.8 66.4 %all-gather.6.cloned.1.call-done = bf16[64,16,1152]{2,1,0:T(8,128)(2,1)} async-done(((bf16[4,16,1152]{2,1,0:T(8,128)(2,1)}), bf16[64,16,1152]{2,1,0:T(8,128)(2,1)}) %all-gather.6.cloned.1.call-update) | async-done | bytes 2359312 | tf_op jit(solution)/shard_map/all_gather | solution.py:58
  102.8 1.2 select_reduce_fusion.2
  105.2 28.7 %all-gather.8.cloned.1.call-done = bf16[16,4,32,1152]{3,2,1,0:T(8,128)(2,1)} async-done(((bf16[16,4,16,1152]{3,2,1,0:T(8,128)(2,1)}), bf16[16,4,32,1152]{3,2,1,0:T(8,128)(2,1)}) %all-gather.8.cloned.1.call-update) | async-done | bytes 4718608 | tf_op jit(solution)/shard_map/all_gather | solution.py:59
  133.9 3.9 %fusion.43 = (bf16[16,1,1,16,1024]{4,3,2,1,0:T(8,128)(2,1)S(1)}, bf16[16,1,1,16,1024]{4,3,2,1,0:T(8,128)(2,1)S(1)}, bf16[16,1,1,16,1024]{4,3,2,1,0:T(8,128)(2,1)...) fusion(bf16[16,4,2,16,1152]{4,3,2,1,0:T(8,128)(2,1)} %bitcast.113), kind=kLoop, calls=%fused_computation.140 | loop fusion | bytes 8388608 | tf_op jit(solution)/shard_map/slice | solution.py:70
  138.3 1.3 fusion.10
  142.0 2.2 fusion.4
  146.2 1.6 maximum_bitcast_fusion
  147.8 4.0 %all-to-all-start.1 = ((f32[4,2,64,1152]{3,2,1,0:T(8,128)}), f32[4,2,64,1152]{3,2,1,0:T(8,128)S(1)}, u32[]{:S(2)}, u32[]{:S(2)}) async-start(f32[4,2,64,1152]{3,2,1,0:T(8,128)} %maximum_bitcast_fusion), calls=%async_computation.1 | async-start | bytes 4718592 | tf_op jit(solution)/shard_map/all_to_all | solution.py:86
  151.9 0.8 slice.231
  155.1 25.5 %all-to-all-done.1 = f32[4,2,64,1152]{3,2,1,0:T(8,128)S(1)} async-done(((f32[4,2,64,1152]{3,2,1,0:T(8,128)}), f32[4,2,64,1152]{3,2,1,0:T(8,128)S(1)}, u32[]{:S(2)}, u32[]{:S(2)}) %all-to-all-start.1) | async-done | bytes 2359328 | tf_op jit(solution)/shard_map/all_to_all | solution.py:86
  183.9 14.5 %all-to-all-start.2 = ((bf16[64,2,640]{2,1,0:T(2,128)(2,1)}), bf16[64,2,640]{2,1,0:T(2,128)(2,1)S(1)}, u32[]{:S(2)}, u32[]{:S(2)}) async-start(bf16[64,2,640]{2,1,0:T(2,128)(2,1)} %reshape.364), calls=%async_computation.2 | async-start | bytes 327680 | tf_op jit(solution)/shard_map/all_to_all | solution.py:217
  203.1 11.4 %all-to-all-done.2 = bf16[64,2,640]{2,1,0:T(2,128)(2,1)S(1)} async-done(((bf16[64,2,640]{2,1,0:T(2,128)(2,1)}), bf16[64,2,640]{2,1,0:T(2,128)(2,1)S(1)}, u32[]{:S(2)}, u32[]{:S(2)}) %all-to-all-start.2) | async-done | bytes 163872 | tf_op jit(solution)/shard_map/all_to_all | solution.py:217
  214.7 5.5 %all-gather.2 = bf16[128,1,1280]{2,0,1:T(8,128)(2,1)S(1)} all-gather(bf16[64,1,1280]{2,0,1:T(8,128)(2,1)S(1)} %copy.103), channel_id=4, replica_groups=mesh['vocab_0'=16,'vocab_1'=4,'vocab_2'=2,'width'=4] {'vocab_2'}, dimensions={0}, use_global_device_ids=true | all-gather | bytes 491520 | tf_op jit(solution)/shard_map/all_gather | solution.py:218
  221.0 3.4 %fusion.27 = (f32[]{:T(128)}, f32[]{:T(128)}, f32[]{:T(128)}, f32[]{:T(128)}, f32[]{:T(128)}, /*index=5*/f32[]{:T(128)}) fusion(f32[128,10]{1,0:T(8,128)S(1)} %slice_add_fusion, f32[]{:T(128)} %get-tuple-element.20, f32[]{:T(128)} %get-tuple-element.21, f32[]{:T(128)} %get-tuple-element.22, f32[]{:T(128)} %get-tuple-element.23), kind=kLoop, calls=%fused_computation.64 | loop fusion | flops 2042 | bytes 5160 | tf_op jit(solution)/shard_map/reduce_sum | solution.py:120
  228.4 2.7 fusion.32
  232.0 4.1 %shard_map.131 = bf16[256,256]{1,0:T(8,128)(2,1)} custom-call(s32[9,128]{1,0:T(8,128)} %get-tuple-element.70.low_ref, s32[9,128]{1,0:T(8,128)} %get-tuple-element.71.high_ref, bf16[128,1152]{1,0:T(8,128)(2,1)} %pad_maximum_fusion.2.terms_ref, bf16[4,128,128]{2,1,0:T(8,128)(2,1)} %weights_ref.1), custom_call_target="tpu_custom_call" | custom-call | tf_op jit(solution)/shard_map/pallas_call | solution.py:166
  236.2 1.6 reduce.27
  238.4 9.1 %all-to-all-start.3 = ((bf16[256,2,128]{2,1,0:T(2,128)(2,1)}), bf16[256,2,128]{2,1,0:T(2,128)(2,1)S(1)}, u32[]{:S(2)}, u32[]{:S(2)}) async-start(bf16[256,2,128]{2,1,0:T(2,128)(2,1)} %reshape.366), calls=%async_computation.3 | async-start | bytes 262144 | tf_op jit(solution)/shard_map/all_to_all | solution.py:226
  247.6 1.3 dynamic-slice
  249.0 0.8 dynamic-update-slice
  249.8 7.4 %all-reduce.1 = f32[4]{0:T(128)S(1)} all-reduce(f32[4]{0:T(128)S(1)} %dynamic-update-slice), channel_id=1, replica_groups=mesh['vocab_0'=16,'vocab_1'=4,'vocab_2'=2,'width'=4] {'width'}, use_global_device_ids=true, to_apply=%add.1 | all-reduce | flops 4 | bytes 32
  257.8 5.5 %all-to-all-done.3 = bf16[256,2,128]{2,1,0:T(2,128)(2,1)S(1)} async-done(((bf16[256,2,128]{2,1,0:T(2,128)(2,1)}), bf16[256,2,128]{2,1,0:T(2,128)(2,1)S(1)}, u32[]{:S(2)}, u32[]{:S(2)}) %all-to-all-start.3) | async-done | bytes 131104 | tf_op jit(solution)/shard_map/all_to_all | solution.py:226
  (130 shorter events, 24.4 us)
Async XLA Ops:
  7.2 92.1 %copy-start.8 = (s32[1024,3]{0,1:T(4,128)S(1)}, s32[1024,3]{0,1:T(4,128)}, u32[]{:S(2)}) copy-start(s32[1024,3]{0,1:T(4,128)} %param.20) | copy-start | bytes 36868
  7.2 92.1 %copy-start.6 = (s32[1024]{0:T(1024)S(1)}, s32[1024]{0:T(1024)}, u32[]{:S(2)}) copy-start(s32[1024]{0:T(1024)} %param.21) | copy-start | bytes 12292
  7.2 94.8 %copy-start.7 = (s32[1280,3]{0,1:T(4,128)S(1)}, s32[1280,3]{0,1:T(4,128)}, u32[]{:S(2)}) copy-start(s32[1280,3]{0,1:T(4,128)} %param.19) | copy-start | bytes 46084
  7.2 92.0 %all-gather.6.cloned.1.call-start = ((), (), s32[]{:S(2)}) async-start(), calls=%async_computation.4 | async-start | bytes 2506752 | tf_op jit(solution)/shard_map/all_gather | solution.py:58
  32.8 101.2 %all-gather.8.cloned.1.call-start = ((), (), s32[]{:S(2)}) async-start(), calls=%async_computation.5 | async-start | bytes 7077888 | tf_op jit(solution)/shard_map/all_gather | solution.py:59
  100.8 2.1 copy-start.9
  133.9 3.9 %copy-start.2 = (bf16[512,2048]{1,0:T(8,128)(2,1)S(1)}, bf16[512,2048]{1,0:T(8,128)(2,1)}, u32[]{:S(2)}) copy-start(bf16[512,2048]{1,0:T(8,128)(2,1)} %param.17) | copy-start | bytes 6291460
  138.3 1.9 copy-start
  141.9 2.4 copy-start.3
  141.9 2.4 copy-start.4
  142.0 3.0 %copy-start.1 = (bf16[640,2048]{1,0:T(8,128)(2,1)S(1)}, bf16[640,2048]{1,0:T(8,128)(2,1)}, u32[]{:S(2)}) copy-start(bf16[640,2048]{1,0:T(8,128)(2,1)} %param.16) | copy-start | bytes 7864324
  147.8 4.0 %copy-start.12 = (s32[4]{0:T(128)S(1)}, s32[4]{0:T(128)}, u32[]{:S(2)}) copy-start(s32[4]{0:T(128)} %dynamic_slice.23) | copy-start | bytes 52
  147.8 4.0 %copy-start.13 = (s32[4]{0:T(128)S(1)}, s32[4]{0:T(128)}, u32[]{:S(2)}) copy-start(s32[4]{0:T(128)} %dynamic_slice.20) | copy-start | bytes 52
  147.8 4.0 %copy-start.14 = (s32[5]{0:T(128)S(1)}, s32[5]{0:T(128)}, u32[]{:S(2)}) copy-start(s32[5]{0:T(128)} %dynamic_slice.22) | copy-start | bytes 64
  147.8 4.0 %copy-start.15 = (s32[5]{0:T(128)S(1)}, s32[5]{0:T(128)}, u32[]{:S(2)}) copy-start(s32[5]{0:T(128)} %dynamic_slice.19) | copy-start | bytes 64
  147.8 6.4 %copy-start.5 = (bf16[4,128,128]{2,1,0:T(8,128)(2,1)S(1)}, bf16[4,128,128]{2,1,0:T(8,128)(2,1)}, u32[]{:S(2)}) copy-start(bf16[4,128,128]{2,1,0:T(8,128)(2,1)} %weights_ref.1) | copy-start | bytes 393220
  147.8 32.8 %all-to-all-start.1 = ((f32[4,2,64,1152]{3,2,1,0:T(8,128)}), f32[4,2,64,1152]{3,2,1,0:T(8,128)S(1)}, u32[]{:S(2)}, u32[]{:S(2)}) async-start(f32[4,2,64,1152]{3,2,1,0:T(8,128)} %maximum_bitcast_fusion), calls=%async_computation.1 | async-start | bytes 4718592 | tf_op jit(solution)/shard_map/all_to_all | solution.py:86
  180.7 18.1 %copy-start.10 = (s32[512]{0:T(512)S(1)}, s32[512]{0:T(512)}, u32[]{:S(2)}) copy-start(s32[512]{0:T(512)} %copy-done.9) | copy-start | bytes 6148
  180.8 19.1 %copy-start.11 = (f32[2]{0:T(128)S(1)}, f32[2]{0:T(128)}, u32[]{:S(2)}) copy-start(f32[2]{0:T(128)} %param.23) | copy-start | bytes 28
  183.9 30.6 %all-to-all-start.2 = ((bf16[64,2,640]{2,1,0:T(2,128)(2,1)}), bf16[64,2,640]{2,1,0:T(2,128)(2,1)S(1)}, u32[]{:S(2)}, u32[]{:S(2)}) async-start(bf16[64,2,640]{2,1,0:T(2,128)(2,1)} %reshape.364), calls=%async_computation.2 | async-start | bytes 327680 | tf_op jit(solution)/shard_map/all_to_all | solution.py:217
  238.4 24.8 %all-to-all-start.3 = ((bf16[256,2,128]{2,1,0:T(2,128)(2,1)}), bf16[256,2,128]{2,1,0:T(2,128)(2,1)S(1)}, u32[]{:S(2)}, u32[]{:S(2)}) async-start(bf16[256,2,128]{2,1,0:T(2,128)(2,1)} %reshape.366), calls=%async_computation.3 | async-start | bytes 262144 | tf_op jit(solution)/shard_map/all_to_all | solution.py:226
Sparse Core Ops, SparseCore 0:
  32.9 66.2 all-gather.5
  101.3 32.6 all-gather.7
where the time goes:
time: 272 us; the launch traced here: 271 us
  waiting for transfers between devices  137 us (50%)
  blocking collectives  36.7 us (13%)
  starting transfers between devices  27.6 us (10%)
  other arithmetic  20.2 us (7%)
  between operations  19.9 us (7%)
  local copies, waits for them, and re-layouts  18 us (7%)
  matrix products  6.99 us (3%)
  Pallas kernels  4.13 us (2%)
    all_gather x1, waiting for transfers between devices, gathered_tiles(): tiles = lax.all_gather(tiles, 'vocab_0')  66.4 us
    all_gather x1, waiting for transfers between devices, gathered_tiles(): return lax.all_gather(tiles, 'vocab_2', axis=2)  28.7 us
    all_to_all x1, waiting for transfers between devices, width_summed(): return jnp.sum(lax.all_to_all(split, 'width', 0, 0, tiled=True), axis=0)  25.5 us
    all_to_all x1, starting transfers between devices, local(): message = lax.all_to_all(message, PLANE, 0, 0, tiled=True)  14.5 us
    all_to_all x1, blocking collectives, gathered_tiles(): lax.all_to_all(jnp.concatenate([parts, codes], axis=2), GROUP, 0, 0, tile...  13.9 us
    all_to_all x1, waiting for transfers between devices, local(): message = lax.all_to_all(message, PLANE, 0, 0, tiled=True)  11.4 us
    all_gather x1, blocking collectives, gathered_tiles(): tiles = lax.all_gather(tile, 'vocab_1')  9.88 us
    all_to_all x1, starting transfers between devices, local(): lax.all_to_all(mixed, ('vocab_0', 'vocab_1', 'width'), 0, 0, tiled=True)  9.14 us
  transfers between devices with their start and end apart: 5, of which 5 were waited for; matrix products, arithmetic and copies ran while one was open for 6% of the time, Pallas kernels for 0%

commit v1 on v0

--- a/solution.py
+++ b/solution.py
@@ -48,42 +48,297 @@
     return jnp.pad(codes.astype(jnp.bfloat16), ((0, 0), (0, BLOCK - 3)))
 
 
-def gathered_tiles(hidden_cat, chosen):
+def column_tile(hidden_cat, chosen):
     rows, columns = hidden_cat.shape
     parts = hidden_cat.reshape(rows, 8, columns // 8).transpose(1, 0, 2)
     codes = jnp.broadcast_to(chosen_codes(chosen)[None], (8, rows, BLOCK))
     tile = lax.all_to_all(jnp.concatenate([parts, codes], axis=2), GROUP, 0, 0, tiled=True)
     tile = tile.reshape(8 * rows, -1)
-    tiles = lax.all_gather(tile, "vocab_1")
-    tiles = lax.all_gather(tiles, "vocab_0")
-    return lax.all_gather(tiles, "vocab_2", axis=2)
-
-
-def partial_logits(tiles, qwen_head, llama_head):
-    chunk = tiles.shape[-1] - BLOCK
-    found = []
-    for tensor in range(4):
-        head = qwen_head if tensor < 2 else llama_head
-        total = 0.0
-        for half in range(2):
-            place = tensor * 2 + half
-            rows = tiles[:, place // 2, place % 2, :, :chunk].reshape(-1, chunk)
-            total = total + lax.dot_general(
-                rows,
-                head[:, half * chunk : (half + 1) * chunk],
-                (((1,), (1,)), ((), ())),
-                preferred_element_type=jnp.float32,
-            )
-        found.append(total)
-    first = jnp.concatenate([found[0], found[2]], axis=1)
-    second = jnp.concatenate([found[1], found[3]], axis=1)
-    return jnp.stack([first, second])
-
-
-def width_summed(partial):
-    steps, rows, entries = partial.shape
-    split = jnp.moveaxis(partial.reshape(steps, rows // 4, 4, entries), 2, 0)
-    return jnp.sum(lax.all_to_all(split, "width", 0, 0, tiled=True), axis=0)
+    return tile[:, :-BLOCK], tile[:, -BLOCK:]
+
+
+def chunk_tensor(y, k):
+    return lax.rem(y + 4 - k, 4)
+
+
+def logits_kernel(
+    tile_ref,
+    code_ref,
+    q_head_ref,
+    l_head_ref,
+    out_ref,
+    codes_ref,
+    held,
+    codes,
+    q_head,
+    l_head,
+    found,
+    parts,
+    sums,
+    head_sem,
+    y_send,
+    y_recv,
+    z_send,
+    z_recv,
+    code_send,
+    code_recv,
+    core_send,
+    core_recv,
+    x_send,
+    x_recv,
+):
+    z, y, c, x = (lax.axis_index(name) for name in ("vocab_0", "vocab_1", "vocab_2", "width"))
+    other = 1 - c
+    z_next = (lax.rem(z + 1, 16), lax.rem(z + 15, 16))
+    x_next = (lax.rem(x + 1, 4), lax.rem(x + 3, 4))
+    chunk = tile_ref.shape[1]
+    q_rows = q_head_ref.shape[0]
+
+    def to(src, dst, send, recv, axis, index):
+        return pltpu.make_async_remote_copy(
+            src_ref=src,
+            dst_ref=dst,
+            send_sem=send,
+            recv_sem=recv,
+            device_id={axis: index},
+            device_id_type=pl.DeviceIdType.MESH,
+        )
+
+    def plane(way, step):
+        return lax.rem(z + 16 - step, 16) if way == 0 else lax.rem(z + step, 16)
+
+    def pair(group):
+        return lax.rem(z + 16 - group, 16), lax.rem(z + jnp.where(group == 8, 0, group), 16)
+
+    def z_copy(way, k, step, src=None):
+        place = held.at[plane(way, step - 1), c, chunk_tensor(y, k)]
+        return to(
+            place if src is None else src,
+            place,
+            z_send.at[way, k, step],
+            z_recv.at[way, k, step],
+            "vocab_0",
+            z_next[way],
+        )
+
+    def z_arrival(way, k, step):
+        place = held.at[plane(way, step), c, chunk_tensor(y, k)]
+        return to(place, place, z_send.at[way, k, step], z_recv.at[way, k, step], "vocab_0", z_next[way])
+
+    def code_copy(way, step, at):
+        place = codes.at[plane(way, at)]
+        return to(
+            place, place, code_send.at[way, step], code_recv.at[way, step], "vocab_0", z_next[way]
+        )
+
+    def core_copy(way, step, at, core):
+        place = held.at[at, core]
+        return to(place, place, core_send.at[way, step], core_recv.at[way, step], "vocab_2", other)
+
+    def x_copy(hop, way, group, src):
+        return to(
+            src,
+            sums.at[hop, way, group],
+            x_send.at[hop, way, group],
+            x_recv.at[hop, way, group],
+            "width",
+            x_next[way],
+        )
+
+    def x_class(way, hop):
+        return lax.rem(x + 7 - hop, 4) if way == 0 else lax.rem(x + 1 + hop, 4)
+
+    head_copies = (
+        pltpu.make_async_copy(q_head_ref, q_head, head_sem.at[0]),
+        pltpu.make_async_copy(l_head_ref, l_head, head_sem.at[1]),
+    )
+    for copy in head_copies:
+        copy.start()
+    barrier = pltpu.get_barrier_semaphore()
+    peers = [("vocab_0", z_next[0]), ("vocab_0", z_next[1]), ("vocab_2", other)]
+    peers += [("vocab_1", lax.rem(y + step, 4)) for step in (1, 2, 3)]
+    peers += [("width", x_next[0]), ("width", x_next[1])]
+    for axis, index in peers:
+        pl.semaphore_signal(
+            barrier, inc=1, device_id={axis: index}, device_id_type=pl.DeviceIdType.MESH
+        )
+    pl.semaphore_wait(barrier, len(peers))
+
+    y_copies = [
+        to(tile_ref, held.at[z, c, y], y_send.at[k], y_recv.at[k], "vocab_1", lax.rem(y + k + 1, 4))
+        for k in range(3)
+    ]
+    for copy in y_copies:
+        copy.start()
+    for way in range(2):
+        z_copy(way, 0, 1, tile_ref).start()
+        to(
+            code_ref,
+            codes.at[z],
+            code_send.at[way, 1],
+            code_recv.at[way, 1],
+            "vocab_0",
+            z_next[way],
+        ).start()
+    held[z, c, y] = tile_ref[...]
+    codes[z] = code_ref[...]
+    for k in range(1, 4):
+        place = held.at[z, c, chunk_tensor(y, k)]
+        to(place, place, y_send.at[k - 1], y_recv.at[k - 1], "vocab_1", y).wait_recv()
+        for way in range(2):
+            z_copy(way, k, 1).start()
+    core_copy(1, 8, z, c).start()
+    for copy in head_copies:
+        copy.wait()
+
+    def step(it, carry):
+        for k in range(4):
+            for way in range(2):
+                last = 8 if (k < 2) == (way == 0) else 7
+
+                @pl.when(it <= last)
+                def _():
+                    z_arrival(way, k, it).wait_recv()
+
+                @pl.when(it < last)
+                def _():
+                    z_copy(way, k, it + 1).start()
+
+        for way in range(2):
+            last = 8 - way
+
+            @pl.when(it <= last)
+            def _():
+                code_copy(way, it, it).wait_recv()
+                core_copy(way, it, plane(way, it), c).start()
+
+            @pl.when(it < last)
+            def _():
+                code_copy(way, it + 1, it).start()
+
+        group = it - 1
+
+        @pl.when((group >= 1) & (group <= 8))
+        def _():
+            low, high = pair(group)
+            core_copy(0, group, low, other).wait_recv()
+            core_copy(1, group, high, other).wait_recv()
+            for model in range(2):
+                head, first = (q_head, 0) if model == 0 else (l_head, q_rows)
+                total = None
+                for half in range(2):
+                    rows = jnp.concatenate(
+                        [held[at, half, 2 * model + s] for s in range(2) for at in (low, high)], axis=0
+                    )
+                    term = lax.dot_general(
+                        rows,
+                        head[:, half * chunk : (half + 1) * chunk],
+                        (((1,), (1,)), ((), ())),
+                        preferred_element_type=jnp.float32,
+                    )
+                    total = term if total is None else total + term
+                for b in range(head.shape[0] // BLOCK):
+                    found[first // BLOCK + b] = total[:, b * BLOCK : (b + 1) * BLOCK]
+            for b in range(B_DEV):
+                for s in range(2):
+                    for turn in range(4):
+                        rows = found[b, pl.ds(32 * s + turn, 8, stride=4), :]
+                        parts[group, s, turn, :, b * BLOCK : (b + 1) * BLOCK] = rows
+            for way in range(2):
+                x_copy(0, way, group, parts.at[group, way, x_class(way, 0)]).start()
+
+        for hop in (1, 2):
+            group_h = it - 1 - hop
+
+            @pl.when((group_h >= 1) & (group_h <= 8))
+            def _():
+                for way in range(2):
+                    place = sums.at[hop - 1, way, group_h]
+                    x_copy(hop - 1, way, group_h, place).wait_recv()
+                    place[...] = place[...] + parts[group_h, way, x_class(way, hop)]
+                    x_copy(hop, way, group_h, place).start()
+
+        group_d = it - 4
+
+        @pl.when((group_d >= 1) & (group_d <= 8))
+        def _():
+            low, high = pair(group_d)
+            for way in range(2):
+                place = sums.at[2, way, group_d]
+                x_copy(2, way, group_d, place).wait_recv()
+                total = place[...] + parts[group_d, way, x]
+                out_ref[way, low] = total[0:4]
+                out_ref[way, high] = total[4:8]
+
+        return carry
+
+    lax.fori_loop(1, 13, step, 0)
+    codes_ref[...] = codes[...]
+
+    for copy in y_copies:
+        copy.wait_send()
+
+    def drain(it, carry):
+        for way in range(2):
+            for k in range(4):
+                last = 8 if (k < 2) == (way == 0) else 7
+
+                @pl.when(it <= last)
+                def _():
+                    z_copy(way, k, it).wait_send()
+
+            last = 8 - way
+
+            @pl.when(it <= last)
+            def _():
+                code_copy(way, it, it).wait_send()
+
+            core_copy(way, it, z, c).wait_send()
+            for hop in range(3):
+                x_copy(hop, way, it, sums.at[0, way, it]).wait_send()
+        return carry
+
+    lax.fori_loop(1, 9, drain, 0)
+
+
+def reduced_logits(tile, code, q_head, l_head):
+    rows, chunk = tile.shape
+    entries = q_head.shape[0] + l_head.shape[0]
+    vmem = pl.BlockSpec(memory_space=pltpu.VMEM)
+    dma = pltpu.SemaphoreType.DMA
+    return pl.pallas_call(
+        logits_kernel,
+        out_shape=(
+            jax.ShapeDtypeStruct((2, 16, 4, entries), jnp.float32),
+            jax.ShapeDtypeStruct((16, rows, BLOCK), jnp.bfloat16),
+        ),
+        in_specs=[vmem, vmem, *[pl.BlockSpec(memory_space=pltpu.HBM)] * 2],
+        out_specs=(vmem, vmem),
+        scratch_shapes=[
+            pltpu.VMEM((16, 2, 4, rows, chunk), jnp.bfloat16),
+            pltpu.VMEM((16, rows, BLOCK), jnp.bfloat16),
+            pltpu.VMEM(q_head.shape, jnp.bfloat16),
+            pltpu.VMEM(l_head.shape, jnp.bfloat16),
+            pltpu.VMEM((B_DEV, 4 * rows, BLOCK), jnp.float32),
+            pltpu.VMEM((9, 2, 4, 8, entries), jnp.float32),
+            pltpu.VMEM((3, 2, 9, 8, entries), jnp.float32),
+            dma((2,)),
+            dma((3,)),
+            dma((3,)),
+            dma((2, 4, 9)),
+            dma((2, 4, 9)),
+            dma((2, 9)),
+            dma((2, 9)),
+            dma((2, 9)),
+            dma((2, 9)),
+            dma((3, 2, 9)),
+            dma((3, 2, 9)),
+        ],
+        compiler_params=pltpu.CompilerParams(
+            collective_id=0, has_side_effects=True, vmem_limit_bytes=40 * 1024 * 1024
+        ),
+        cost_estimate=pl.CostEstimate(flops=3 * 10**10, bytes_accessed=10**7, transcendentals=0),
+    )(tile, code, q_head, l_head)
 
 
 def row_message(logits, chosen_pos, chosen_col, own_low, own_high, align_weights):
@@ -193,8 +448,9 @@
     hidden_cat = jnp.concatenate(
         [qwen_hidden, qwen_next_hidden, llama_hidden, llama_next_hidden], axis=1
     )
-    tiles = gathered_tiles(hidden_cat, chosen)
-    codes = tiles[:, 0, 0, :, -BLOCK:][:, :, :3].astype(jnp.int32).reshape(-1, 4, 3)
+    logits, codes = reduced_logits(*column_tile(hidden_cat, chosen), qwen_head, llama_head)
+    logits = logits.reshape(2, -1, B_DEV * BLOCK)
+    codes = codes[:, :, :3].astype(jnp.int32).reshape(-1, 4, 3)
     codes = lax.dynamic_index_in_dim(codes, width, 1, keepdims=False)
     chosen_pos = positions_of(union_order, codes[:, 0] * 32 + codes[:, 1])
     q_low, q_high = link_codes(qwen_links, union_order, qwen_links.shape[0] // 2)
@@ -212,7 +468,6 @@
         jnp.concatenate([by_source(q, QB_DEV), by_source(l, LB_DEV)])
         for q, l in ((q_low, l_low), (q_high, l_high))
     )
-    logits = width_summed(partial_logits(tiles, qwen_head, llama_head))
     message = row_message(logits, chosen_pos, codes[:, 2], own_low, own_high, align_weights)
     message = lax.all_to_all(message, PLANE, 0, 0, tiled=True)
     message = lax.all_gather(message, "vocab_2", axis=0, tiled=True)

time: 272 us -> 163 us (0.60)
  waiting for transfers between devices: 137 us -> 16 us
  Pallas kernels: 4.13 us -> 61.8 us
  blocking collectives: 36.7 us -> 14.3 us
  between operations: 19.9 us -> 6.22 us
  matrix products: 6.99 us -> 0.2 us
  local copies, waits for them, and re-layouts: 18 us -> 14.4 us
    all_gather x2 -> x0, waiting for transfers between devices: 95.1 us -> none  [the longest x1 66.4 us: gathered_tiles(): tiles = lax.all_gather(tiles, 'vocab_0')]
    pallas_call x0 -> x1, Pallas kernels: none -> 57.7 us  [reduced_logits(): pl.pallas_call(logits_kernel, out_shape=(jax.ShapeDtypeStruct((2, 16, 4,...]
    all_to_all x1, waiting for transfers between devices: 25.5 us -> 0.01 us  [column_tile(): lax.all_to_all(jnp.concatenate([parts, codes], axis=2), GROUP, 0, 0, tile...]
    all_to_all x1 -> x0, blocking collectives: 13.9 us -> none  [gathered_tiles(): lax.all_to_all(jnp.concatenate([parts, codes], axis=2), GROUP, 0, 0, tile...]
    all_gather x1 -> x0, blocking collectives: 9.88 us -> none  [gathered_tiles(): tiles = lax.all_gather(tile, 'vocab_1')]
    dot_general x8 -> x0, matrix products: 6.78 us -> none  [partial_logits(): lax.dot_general(rows, head[:, half * chunk:(half + 1) * chunk], (((1,), (...]
    all_to_all x1, starting transfers between devices: 14.5 us -> 8.31 us  [local(): message = lax.all_to_all(message, PLANE, 0, 0, tiled=True)]
    all_to_all x1, starting transfers between devices: 3.95 us -> 10.1 us  [column_tile(): lax.all_to_all(jnp.concatenate([parts, codes], axis=2), GROUP, 0, 0, tile...]
  transfers between devices with their start and end apart: 5 -> 3, of which waited for: 5 -> 2; matrix products, arithmetic and copies ran while one was open for 6% -> 8% of each run, Pallas kernels for 0% -> 0%
where the time goes in v1:
time: 163 us; the launch traced here: 161 us
  Pallas kernels  61.8 us (38%)
  starting transfers between devices  28.2 us (17%)
  other arithmetic  20.3 us (12%)
  waiting for transfers between devices  16 us (10%)
  local copies, waits for them, and re-layouts  14.4 us (9%)
  blocking collectives  14.3 us (9%)
  between operations  6.22 us (4%)
    pallas_call x1, Pallas kernels, reduced_logits(): pl.pallas_call(logits_kernel, out_shape=(jax.ShapeDtypeStruct((2, 16, 4,...  57.7 us
    all_to_all x1, waiting for transfers between devices, local(): message = lax.all_to_all(message, PLANE, 0, 0, tiled=True)  10.9 us
    all_to_all x1, starting transfers between devices, column_tile(): lax.all_to_all(jnp.concatenate([parts, codes], axis=2), GROUP, 0, 0, tile...  10.1 us
    all_to_all x1, starting transfers between devices, local(): lax.all_to_all(mixed, ('vocab_0', 'vocab_1', 'width'), 0, 0, tiled=True)  9.75 us
    all_to_all x1, starting transfers between devices, local(): message = lax.all_to_all(message, PLANE, 0, 0, tiled=True)  8.31 us
    unnamed x1, blocking collectives  7.49 us
    unnamed x19, local copies, waits for them, and re-layouts  7.27 us
    all_gather x1, blocking collectives, local(): message = lax.all_gather(message, 'vocab_2', axis=0, tiled=True)  6.83 us
  transfers between devices with their start and end apart: 3, of which 2 were waited for; matrix products, arithmetic and copies ran while one was open for 8% of the time, Pallas kernels for 0%

profile of v1, /device:TPU:1, one launch (start us, length us, event | category | flops | bytes accessed | tf_op | source)
XLA Modules:
  0.0 161.4 jit_solution(7698962994459502220)
XLA Ops:
  1.5 0.8 pad_maximum_fusion.2
  2.9 10.1 %all-to-all-start = ((bf16[8,2,1152]{2,1,0:T(2,128)(2,1)}), bf16[8,2,1152]{2,1,0:T(2,128)(2,1)S(1)}, u32[]{:S(2)}, u32[]{:S(2)}) async-start(bf16[8,2,1152]{2,1,0:T(2,128)(2,1)} %pad_maximum_fusion.1), calls=%async_computation | async-start | bytes 73728 | tf_op jit(solution)/shard_map/all_to_all | solution.py:55
  13.0 0.8 fusion.31
  13.8 1.4 select_reduce_fusion.1
  15.2 0.8 select_reduce_fusion.4
  16.2 0.9 slice_reduce_fusion.10
  17.0 1.5 select_reduce_fusion
  18.6 1.2 select_reduce_fusion.2
  20.1 1.7 %copy-done = bf16[640,2048]{1,0:T(8,128)(2,1)S(1)} copy-done((bf16[640,2048]{1,0:T(8,128)(2,1)S(1)}, bf16[640,2048]{1,0:T(8,128)(2,1)}, u32[]{:S(2)}) %copy-start) | copy-done | bytes 2621464
  21.8 1.6 copy-done.1
  23.4 57.7 %shard_map.131 = (f32[2,16,4,1152]{3,2,1,0:T(4,128)S(1)}, bf16[16,16,128]{2,1,0:T(8,128)(2,1)S(1)}) custom-call(bf16[16,1024]{1,0:T(8,128)(2,1)S(1)} %slice.172.tile_ref, bf16[16,128]{1,0:T(8,128)(2,1)S(1)} %slice.173.code_ref, bf16[640,2048]{1,0:T(8,128)(2,1)S(1)} %copy-done, bf16[512,2048]{1,0:T(8,128)(2,1)S(1)} %copy-done.1), custom_call_target="tpu_custom_call" | custom-call | flops 30000001024 | bytes 10000000 | tf_op jit(solution)/shard_map/pallas_call | solution.py:309
  86.2 8.3 %all-to-all-start.1 = ((bf16[64,2,640]{2,1,0:T(2,128)(2,1)}), bf16[64,2,640]{2,1,0:T(2,128)(2,1)S(1)}, u32[]{:S(2)}, u32[]{:S(2)}) async-start(bf16[64,2,640]{2,1,0:T(2,128)(2,1)} %reshape.363), calls=%async_computation.1 | async-start | bytes 327680 | tf_op jit(solution)/shard_map/all_to_all | solution.py:472
  99.3 10.9 %all-to-all-done.1 = bf16[64,2,640]{2,1,0:T(2,128)(2,1)S(1)} async-done(((bf16[64,2,640]{2,1,0:T(2,128)(2,1)}), bf16[64,2,640]{2,1,0:T(2,128)(2,1)S(1)}, u32[]{:S(2)}, u32[]{:S(2)}) %all-to-all-start.1) | async-done | bytes 163872 | tf_op jit(solution)/shard_map/all_to_all | solution.py:472
  110.4 6.8 %all-gather = bf16[128,1,1280]{2,0,1:T(8,128)(2,1)S(1)} all-gather(bf16[64,1,1280]{2,0,1:T(8,128)(2,1)S(1)} %copy.83), channel_id=2, replica_groups=mesh['vocab_0'=16,'vocab_1'=4,'vocab_2'=2,'width'=4] {'vocab_2'}, dimensions={0}, use_global_device_ids=true | all-gather | bytes 491520 | tf_op jit(solution)/shard_map/all_gather | solution.py:473
  118.0 3.4 %fusion.15 = (f32[]{:T(128)}, f32[]{:T(128)}, f32[]{:T(128)}, f32[]{:T(128)}, f32[]{:T(128)}, /*index=5*/f32[]{:T(128)}) fusion(f32[128,10]{1,0:T(8,128)S(1)} %slice_add_fusion, f32[]{:T(128)} %get-tuple-element.24, f32[]{:T(128)} %get-tuple-element.25, f32[]{:T(128)} %get-tuple-element.26, f32[]{:T(128)} %get-tuple-element.27), kind=kLoop, calls=%fused_computation.44 | loop fusion | flops 2042 | bytes 5160 | tf_op jit(solution)/shard_map/reduce_sum | solution.py:375
  125.4 2.7 %fusion.20 = (f32[128]{0:T(128)S(1)}, f32[128]{0:T(128)S(1)}) fusion(f32[128,10]{1,0:T(8,128)S(1)} %slice_add_fusion, f32[]{:T(128)} %get-tuple-element.18, f32[]{:T(128)} %get-tuple-element.24, f32[]{:T(128)S(6)} %mul.265, f32[]{:T(128)} %get-tuple-element.19, f32[]{:T(128)} %get-tuple-element.25, f32[]{:T(128)S(6)} %mul.272), kind=kLoop, calls=%fused_computation.61 | loop fusion | flops 768 | bytes 2072 | tf_op jit(solution)/shard_map/div | solution.py:391
  129.1 4.1 %shard_map.132 = bf16[256,256]{1,0:T(8,128)(2,1)} custom-call(s32[9,128]{1,0:T(8,128)} %get-tuple-element.66.low_ref, s32[9,128]{1,0:T(8,128)} %get-tuple-element.67.high_ref, bf16[128,1152]{1,0:T(8,128)(2,1)} %pad_maximum_fusion.terms_ref, bf16[4,128,128]{2,1,0:T(8,128)(2,1)} %weights_ref.1), custom_call_target="tpu_custom_call" | custom-call | tf_op jit(solution)/shard_map/pallas_call | solution.py:421
  133.2 1.6 reduce.25
  135.5 9.8 %all-to-all-start.2 = ((bf16[256,2,128]{2,1,0:T(2,128)(2,1)}), bf16[256,2,128]{2,1,0:T(2,128)(2,1)S(1)}, u32[]{:S(2)}, u32[]{:S(2)}) async-start(bf16[256,2,128]{2,1,0:T(2,128)(2,1)} %reshape.365), calls=%async_computation.2 | async-start | bytes 262144 | tf_op jit(solution)/shard_map/all_to_all | solution.py:481
  145.2 1.3 dynamic-slice
  146.7 0.8 dynamic-update-slice
  147.5 7.5 %all-reduce.1 = f32[4]{0:T(128)S(1)} all-reduce(f32[4]{0:T(128)S(1)} %dynamic-update-slice), channel_id=1, replica_groups=mesh['vocab_0'=16,'vocab_1'=4,'vocab_2'=2,'width'=4] {'width'}, use_global_device_ids=true, to_apply=%add.1 | all-reduce | flops 4 | bytes 32
  155.5 5.0 %all-to-all-done.2 = bf16[256,2,128]{2,1,0:T(2,128)(2,1)S(1)} async-done(((bf16[256,2,128]{2,1,0:T(2,128)(2,1)}), bf16[256,2,128]{2,1,0:T(2,128)(2,1)S(1)}, u32[]{:S(2)}, u32[]{:S(2)}) %all-to-all-start.2) | async-done | bytes 131104 | tf_op jit(solution)/shard_map/all_to_all | solution.py:481
  160.6 0.8 log_bitcast_fusion
  (84 shorter events, 13.7 us)
Async XLA Ops:
  2.9 17.1 %all-to-all-start = ((bf16[8,2,1152]{2,1,0:T(2,128)(2,1)}), bf16[8,2,1152]{2,1,0:T(2,128)(2,1)S(1)}, u32[]{:S(2)}, u32[]{:S(2)}) async-start(bf16[8,2,1152]{2,1,0:T(2,128)(2,1)} %pad_maximum_fusion.1), calls=%async_computation | async-start | bytes 73728 | tf_op jit(solution)/shard_map/all_to_all | solution.py:55
  20.1 1.7 %copy-start = (bf16[640,2048]{1,0:T(8,128)(2,1)S(1)}, bf16[640,2048]{1,0:T(8,128)(2,1)}, u32[]{:S(2)}) copy-start(bf16[640,2048]{1,0:T(8,128)(2,1)} %q_head_ref.1) | copy-start | bytes 7864324
  21.8 1.6 copy-start.1
  23.4 58.3 %copy-start.3 = (s32[1024]{0:T(1024)S(1)}, s32[1024]{0:T(1024)}, u32[]{:S(2)}) copy-start(s32[1024]{0:T(1024)} %param.21) | copy-start | bytes 12292
  23.4 59.0 %copy-start.2 = (bf16[4,128,128]{2,1,0:T(8,128)(2,1)S(1)}, bf16[4,128,128]{2,1,0:T(8,128)(2,1)}, u32[]{:S(2)}) copy-start(bf16[4,128,128]{2,1,0:T(8,128)(2,1)} %weights_ref.1) | copy-start | bytes 393220
  82.4 13.7 %copy-start.4 = (f32[2]{0:T(128)S(1)}, f32[2]{0:T(128)}, u32[]{:S(2)}) copy-start(f32[2]{0:T(128)} %param.23) | copy-start | bytes 28
  86.2 24.0 %all-to-all-start.1 = ((bf16[64,2,640]{2,1,0:T(2,128)(2,1)}), bf16[64,2,640]{2,1,0:T(2,128)(2,1)S(1)}, u32[]{:S(2)}, u32[]{:S(2)}) async-start(bf16[64,2,640]{2,1,0:T(2,128)(2,1)} %reshape.363), calls=%async_computation.1 | async-start | bytes 327680 | tf_op jit(solution)/shard_map/all_to_all | solution.py:472
  135.5 25.1 %all-to-all-start.2 = ((bf16[256,2,128]{2,1,0:T(2,128)(2,1)}), bf16[256,2,128]{2,1,0:T(2,128)(2,1)S(1)}, u32[]{:S(2)}, u32[]{:S(2)}) async-start(bf16[256,2,128]{2,1,0:T(2,128)(2,1)} %reshape.365), calls=%async_computation.2 | async-start | bytes 262144 | tf_op jit(solution)/shard_map/all_to_all | solution.py:481

commit v2 on v0

v2 whole, which is shorter than its diff:
```python
import functools

import jax
import jax.numpy as jnp
from jax import lax
from jax.experimental import pallas as pl
from jax.experimental.pallas import tpu as pltpu
from jax.sharding import Mesh
from jax.sharding import PartitionSpec as P

BLOCK = 128
QB_DEV = 5
LB_DEV = 4
B_DEV = QB_DEV + LB_DEV
KINDS = 4
UBLOCKS = 1024
SMOOTHING = 0.01
UNIFORM = SMOOTHING / (UBLOCKS * BLOCK)
VOCAB = ("vocab_0", "vocab_1", "vocab_2")
PLANE = ("vocab_0", "vocab_1")
GROUP = ("vocab_1", "vocab_2")


def positions_of(union_order, blocks):
    places = jnp.arange(UBLOCKS, dtype=jnp.int32)
    return jnp.sum(jnp.where(union_order[None, :] == blocks[:, None], places[None, :], 0), axis=1)


def link_codes(links, union_order, blocks):
    codes = positions_of(union_order, links[:, 1]) * KINDS + links[:, 2]
    hit = links[:, 0][None, :] == jnp.arange(blocks, dtype=jnp.int32)[:, None]
    low = jnp.min(jnp.where(hit, codes[None, :], UBLOCKS * KINDS), axis=1)
    high = jnp.max(jnp.where(hit, codes[None, :], -1), axis=1)
    return low, high


def own_codes(links, first, blocks):
    codes = links[:, 1] * KINDS + links[:, 2]
    hit = links[:, 0][None, :] == (first + jnp.arange(blocks, dtype=jnp.int32))[:, None]
    low = jnp.min(jnp.where(hit, codes[None, :], UBLOCKS * KINDS), axis=1)
    high = jnp.max(jnp.where(hit, codes[None, :], -1), axis=1)
    return low, high


def chosen_codes(chosen):
    block = chosen // BLOCK
    codes = jnp.stack([block // 32, block % 32, chosen % BLOCK], axis=1)
    return jnp.pad(codes.astype(jnp.bfloat16), ((0, 0), (0, BLOCK - 3)))


def column_tile(hidden_cat, chosen):
    rows, columns = hidden_cat.shape
    parts = hidden_cat.reshape(rows, 8, columns // 8).transpose(1, 0, 2)
    codes = jnp.broadcast_to(chosen_codes(chosen)[None], (8, rows, BLOCK))
    tile = lax.all_to_all(jnp.concatenate([parts, codes], axis=2), GROUP, 0, 0, tiled=True)
    tile = tile.reshape(8 * rows, -1)
    return tile[:, :-BLOCK], tile[:, -BLOCK:]


def chunk_tensor(y, k):
    return lax.rem(y + 4 - k, 4)


def ensemble_kernel(
    tile_ref,
    code_ref,
    own_ref,
    low_ref,
    high_ref,
    weights_ref,
    prior_ref,
    q_head_ref,
    l_head_ref,
    out_ref,
    lik_ref,
    held,
    codes,
    q_head,
    l_head,
    found,
    parts,
    sums,
    lines,
    sent,
    got,
    terms,
    mixed_out,
    mixed_in,
    lik_out,
    lik_in,
    owned_out,
    owned_in,
    turned,
    head_sem,
    y_send,
    y_recv,
    z_send,
    z_recv,
    code_send,
    code_recv,
    core_send,
    core_recv,
    x_send,
    x_recv,
    row_send,
    row_recv,
    swap_send,
    swap_recv,
    mix_send,
    mix_recv,
    end_send,
    end_recv,
):
    z, y, c, x = (lax.axis_index(name) for name in ("vocab_0", "vocab_1", "vocab_2", "width"))
    other = 1 - c
    z_next = (lax.rem(z + 1, 16), lax.rem(z + 15, 16))
    x_next = (lax.rem(x + 1, 4), lax.rem(x + 3, 4))
    chunk = tile_ref.shape[1]
    f32, bf16 = jnp.float32, jnp.bfloat16

    def to(src, dst, send, recv, device):
        return pltpu.make_async_remote_copy(
            src_ref=src,
            dst_ref=dst,
            send_sem=send,
            recv_sem=recv,
            device_id=device,
            device_id_type=pl.DeviceIdType.MESH,
        )

    def plane(way, step):
        return lax.rem(z + 16 - step, 16) if way == 0 else lax.rem(z + step, 16)

    def pair(group):
        return lax.rem(z + 16 - group, 16), lax.rem(z + jnp.where(group == 8, 0, group), 16)

    def z_copy(way, k, step, src=None):
        place = held.at[plane(way, step - 1), c, chunk_tensor(y, k)]
        src = place if src is None else src
        return to(src, place, z_send.at[way, k, step], z_recv.at[way, k, step], {"vocab_0": z_next[way]})

    def z_arrival(way, k, step):
        place = held.at[plane(way, step), c, chunk_tensor(y, k)]
        return to(place, place, z_send.at[way, k, step], z_recv.at[way, k, step], {"vocab_0": z_next[way]})

    def code_copy(way, step, at):
        place = codes.at[plane(way, at)]
        return to(place, place, code_send.at[way, step], code_recv.at[way, step], {"vocab_0": z_next[way]})

    def core_copy(way, step, at, core):
        place = held.at[at, core]
        return to(place, place, core_send.at[way, step], core_recv.at[way, step], {"vocab_2": other})

    def x_copy(hop, way, group, src):
        dst = sums.at[hop, way, group]
        send, recv = x_send.at[hop, way, group], x_recv.at[hop, way, group]
        return to(src, dst, send, recv, {"width": x_next[way]})

    def x_class(way, hop):
        return lax.rem(x + 7 - hop, 4) if way == 0 else lax.rem(x + 1 + hop, 4)

    def row_copy(dz, dy, at_z, at_y):
        send, recv = row_send.at[dz, dy], row_recv.at[dz, dy]
        device = {"vocab_0": at_z, "vocab_1": at_y}
        return to(sent.at[at_z, at_y], got.at[c, z, y], send, recv, device)

    def end_copy(dz, dy, at_z, at_y):
        send, recv = end_send.at[dz, dy], end_recv.at[dz, dy]
        device = {"vocab_0": at_z, "vocab_1": at_y}
        return to(owned_out.at[at_z, at_y], owned_in.at[z, y], send, recv, device)

    def mix_copies(dx, t):
        to_x = lax.rem(x + dx, 4)
        send, recv = mix_send.at[t, dx], mix_recv.at[t, dx]
        if t == 2:
            return to(lik_out, lik_in.at[x], send, recv, {"width": to_x})
        return to(mixed_out.at[t, to_x], mixed_in.at[t, x], send, recv, {"width": to_x})

    head_copies = (
        pltpu.make_async_copy(q_head_ref, q_head, head_sem.at[0]),
        pltpu.make_async_copy(l_head_ref, l_head, head_sem.at[1]),
    )
    for copy in head_copies:
        copy.start()
    barrier = pltpu.get_barrier_semaphore()
    peers = [{"vocab_0": z_next[0]}, {"vocab_0": z_next[1]}, {"vocab_2": other}]
    peers += [{"vocab_1": lax.rem(y + step, 4)} for step in (1, 2, 3)]
    peers += [{"width": lax.rem(x + step, 4)} for step in (1, 2, 3)]
    for device in peers:
        pl.semaphore_signal(barrier, inc=1, device_id=device, device_id_type=pl.DeviceIdType.MESH)
    pl.semaphore_wait(barrier, len(peers))

    y_copies = [
        to(
            tile_ref,
            held.at[z, c, y],
            y_send.at[k],
            y_recv.at[k],
            {"vocab_1": lax.rem(y + k + 1, 4)},
        )
        for k in range(3)
    ]
    for copy in y_copies:
        copy.start()
    for way in range(2):
        z_copy(way, 0, 1, tile_ref).start()
        send, recv = code_send.at[way, 1], code_recv.at[way, 1]
        to(code_ref, codes.at[z], send, recv, {"vocab_0": z_next[way]}).start()
    held[z, c, y] = tile_ref[...]
    codes[z] = code_ref[...]
    lines[...] = jnp.zeros(lines.shape, f32)
    for k in range(1, 4):
        place = held.at[z, c, chunk_tensor(y, k)]
        to(place, place, y_send.at[k - 1], y_recv.at[k - 1], {"vocab_1": lax.rem(y + k, 4)}).wait_recv()
        for way in range(2):
            z_copy(way, k, 1).start()
    core_copy(1, 8, z, c).start()
    for copy in head_copies:
        copy.wait()

    def multiply(group, model):
        low, high = pair(group)
        head, first = ((q_head, 0), (l_head, QB_DEV))[model]
        total = None
        for half in range(2):
            rows = jnp.concatenate(
                [held[at, half, 2 * model + s] for s in range(2) for at in (low, high)], axis=0
            )
            term = lax.dot_general(
                rows,
                head[:, half * chunk : (half + 1) * chunk],
                (((1,), (1,)), ((), ())),
                preferred_element_type=f32,
            )
            total = term if total is None else total + term
        for b in range(head.shape[0] // BLOCK):
            found[first + b] = total[:, b * BLOCK : (b + 1) * BLOCK]

    def split_rows(group):
        for b in range(B_DEV):
            for s in range(2):
                for turn in range(4):
                    rows = found[b, pl.ds(32 * s + turn, 8, stride=4), :]
                    parts[group, s, turn, :, b * BLOCK : (b + 1) * BLOCK] = rows

    def chosen_weights(low, high):
        for n, at in enumerate((low, high)):
            turned[16 * n : 16 * (n + 1), :] = codes[at].astype(f32)
        picked = turned[pl.ds(x, 8, stride=4), :]
        block = picked[:, 0:1] * 32.0 + picked[:, 1:2]
        lane = lax.broadcasted_iota(jnp.int32, (8, BLOCK), 1)
        one_hot = jnp.where(picked[:, 2:3] == lane.astype(f32), 1.0, 0.0).astype(bf16)
        weight = [jnp.zeros((8, BLOCK), f32) for _ in range(B_DEV)]
        for kind in range(KINDS):
            column = lax.dot_general(
                one_hot, weights_ref[kind], (((1,), (1,)), ((), ())), preferred_element_type=f32
            )
            code = block * KINDS + kind
            for b in range(B_DEV):
                count = jnp.where(own_ref[b : b + 1, :] == code, 1.0, 0.0) + jnp.where(
                    own_ref[16 + b : 17 + b, :] == code, 1.0, 0.0
                )
                weight[b] += count * column
        return weight

    def message_rows(group, totals):
        low, high = pair(group)
        weight = chosen_weights(low, high)
        spans = ((0, QB_DEV), (QB_DEV, B_DEV))
        values = []
        for s in range(2):
            for first, last in spans:
                part = totals[s][:, first * BLOCK : last * BLOCK]
                top = jnp.max(part, axis=1, keepdims=True)
                powers = jnp.exp(part - top)
                values += [top, jnp.sum(powers, axis=1, keepdims=True)]
                pieces = [powers[:, b * BLOCK : (b + 1) * BLOCK] for b in range(last - first)]
                if s == 0:
                    value = sum(piece * weight[first + b] for b, piece in enumerate(pieces))
                    values.append(jnp.sum(value, axis=1, keepdims=True))
                else:
                    for b, piece in enumerate(pieces):
                        for n, at in enumerate((low, high)):
                            lines[pl.ds(at * 64 + first + b, 4, stride=16), :] = piece[4 * n : 4 * n + 4]
        lane = lax.broadcasted_iota(jnp.int32, (8, BLOCK), 1)
        rest = jnp.zeros((8, BLOCK), f32)
        for n, value in enumerate(values):
            rest = jnp.where(lane == n, value, rest)
        for row in range(3):
            part = rest.astype(bf16).astype(f32)
            rest = rest - part
            for n, at in enumerate((low, high)):
                lines[pl.ds(at * 64 + B_DEV + row, 4, stride=16), :] = part[4 * n : 4 * n + 4]
        for at in (low, high):
            rows = lines[pl.ds(pl.multiple_of(at * 64, 64), 64), :]
            sent[at] = rows.astype(bf16).reshape(4, 16, BLOCK)
        for way, at in enumerate((low, high)):
            for dy in range(4):
                to_y = lax.rem(y + dy, 4)
                if way == 0:
                    row_copy(16 - group, dy, at, to_y).start()
                else:
                    dz = jnp.where(group == 8, 0, group)
                    if dy:
                        row_copy(dz, dy, at, to_y).start()
                    else:

                        @pl.when(group < 8)
                        def _():
                            row_copy(dz, dy, at, to_y).start()

    def step(it, carry):
        def on_group(group, run):
            pl.when((group >= 1) & (group <= 8))(run)

        def forward(k):
            for way in range(2):
                last = 8 if (k < 2) == (way == 0) else 7

                @pl.when(it <= last)
                def _():
                    z_arrival(way, k, it).wait_recv()

                @pl.when(it < last)
                def _():
                    z_copy(way, k, it + 1).start()

        def first_hop():
            group = it - 1
            split_rows(group)
            for way in range(2):
                x_copy(0, way, group, parts.at[group, way, x_class(way, 0)]).start()

        def next_hop(hop):
            group = it - 1 - hop
            for way in range(2):
                place = sums.at[hop - 1, way, group]
                x_copy(hop - 1, way, group, place).wait_recv()
                place[...] = place[...] + parts[group, way, x_class(way, hop)]
                x_copy(hop, way, group, place).start()

        def last_hop():
            group = it - 4
            totals = []
            for way in range(2):
                place = sums.at[2, way, group]
                x_copy(2, way, group, place).wait_recv()
                totals.append(place[...] + parts[group, way, x])
            message_rows(group, totals)

        def arrived():
            low, high = pair(it - 1)
            core_copy(0, it - 1, low, other).wait_recv()
            core_copy(1, it - 1, high, other).wait_recv()
            multiply(it - 1, 0)

        forward(0)
        on_group(it - 1, arrived)
        forward(1)
        on_group(it - 1, lambda: multiply(it - 1, 1))
        forward(2)
        on_group(it - 1, first_hop)
        on_group(it - 2, lambda: next_hop(1))
        on_group(it - 3, lambda: next_hop(2))
        forward(3)
        for way in range(2):
            last = 8 - way

            @pl.when(it <= last)
            def _():
                core_copy(way, it, plane(way, it), c).start()
                code_copy(way, it, it).wait_recv()

            @pl.when(it < last)
            def _():
                code_copy(way, it + 1, it).start()

        on_group(it - 4, last_hop)
        return carry

    lax.fori_loop(1, 13, step, 0)

    got[c, z, y] = sent[z, y]

    def others(run):
        def visit(i, carry):
            dz, dy = i // 4, lax.rem(i, 4)
            run(dz, dy)
            return carry

        lax.fori_loop(1, 64, visit, 0)

    def row_arrival(dz, dy):
        at_z, at_y = lax.rem(z + 16 - dz, 16), lax.rem(y + 4 - dy, 4)
        place = got.at[c, at_z, at_y]
        to(place, place, row_send.at[dz, dy], row_recv.at[dz, dy], {"vocab_0": at_z}).wait_recv()

    others(row_arrival)
    swap = to(got.at[c], got.at[c], swap_send, swap_recv, {"vocab_2": other})
    swap.start()
    to(got.at[other], got.at[other], swap_send, swap_recv, {"vocab_2": other}).wait_recv()
    terms[...] = got[...].reshape(terms.shape).astype(f32)

    stats = terms[pl.ds(B_DEV, 128, stride=16), :]
    for row in range(1, 3):
        stats = stats + terms[pl.ds(B_DEV + row, 128, stride=16), :]
    highest = jnp.max(stats, axis=0, keepdims=True)

    def share(n):
        factor = jnp.exp(stats[:, n : n + 1] - highest[:, n : n + 1])
        return factor, jnp.sum(factor * stats[:, n + 1 : n + 2], axis=0, keepdims=True)

    masses = []
    for model in range(2):
        factor, total = share(3 * model)
        value = jnp.sum(factor * stats[:, 3 * model + 2 : 3 * model + 3], axis=0, keepdims=True)
        value = 0.5 * value / total
        prior = prior_ref[model : model + 1, 0:1]
        masses.append(prior * ((1.0 - SMOOTHING) * value + UNIFORM))
    together = masses[0] + masses[1]
    lik_out[...] = jnp.broadcast_to(jnp.log(together), lik_out.shape)
    for dx in range(1, 4):
        mix_copies(dx, 2).start()
    scales = []
    for model in range(2):
        factor, total = share(6 + 2 * model)
        scales.append(factor * ((masses[model] / together) * 0.5 / total))
    for b in range(B_DEV):
        rows = terms[pl.ds(b, 128, stride=16), :]
        scaled = rows * scales[0 if b < QB_DEV else 1]
        found_b = scaled.astype(bf16)
        sent_b = (b * 128, (b + 1) * 128)
        turned[sent_b[0] : sent_b[1], :] = found_b.astype(f32)

    spot = lax.broadcasted_iota(jnp.int32, (256, BLOCK), 0)
    first = (16 * lax.rem(spot, 64) + 8 * c + 2 * (spot // 64)) * KINDS
    for t in range(2):
        mixed = jnp.zeros((256, BLOCK), f32)
        for kind in range(KINDS):
            code = first + (t * KINDS + kind)
            total = jnp.zeros((256, BLOCK), f32)
            for b in range(B_DEV):
                hits = jnp.where(low_ref[b : b + 1, :] == code, 1.0, 0.0) + jnp.where(
                    high_ref[b : b + 1, :] == code, 1.0, 0.0
                )
                total += jnp.dot(
                    hits.astype(bf16),
                    turned[b * 128 : (b + 1) * 128, :].astype(bf16),
                    preferred_element_type=f32,
                )
            mixed += jnp.dot(total.astype(bf16), weights_ref[kind], preferred_element_type=f32)
        mixed_out[t] = mixed.astype(bf16).reshape(4, 64, BLOCK)
        for dx in range(1, 4):
            mix_copies(dx, t).start()
        mixed_in[t, x] = mixed_out[t, x]
    lik_in[x] = lik_out[...]
    for dx in range(1, 4):
        from_x = lax.rem(x + 4 - dx, 4)
        for t in range(3):
            place = lik_in.at[from_x] if t == 2 else mixed_in.at[t, from_x]
            to(place, place, mix_send.at[t, dx], mix_recv.at[t, dx], {"width": from_x}).wait_recv()
    for t in range(2):
        for w in range(4):
            lines[pl.ds(w * 2 + t, 64, stride=8), :] = mixed_in[t, w].astype(f32)
    owned_out[...] = lines[0:512, :].reshape(16, 4, 8, BLOCK).astype(bf16)

    def end_start(dz, dy):
        end_copy(dz, dy, lax.rem(z + dz, 16), lax.rem(y + dy, 4)).start()

    def end_arrival(dz, dy):
        at_z, at_y = lax.rem(z + 16 - dz, 16), lax.rem(y + 4 - dy, 4)
        place = owned_in.at[at_z, at_y]
        to(place, place, end_send.at[dz, dy], end_recv.at[dz, dy], {"vocab_0": at_z}).wait_recv()

    others(end_start)
    owned_in[z, y] = owned_out[z, y]
    lik_ref[...] = lik_in[...]
    others(end_arrival)
    turned[0:512, :] = owned_in[...].astype(f32).reshape(512, BLOCK)
    for t in range(2):
        rows = turned[pl.ds(t, 256, stride=2), :]
        out_ref[:, t * BLOCK : (t + 1) * BLOCK] = jnp.log((1.0 - SMOOTHING) * rows + UNIFORM)

    for copy in y_copies:
        copy.wait_send()

    def drain(it, carry):
        for way in range(2):
            for k in range(4):
                last = 8 if (k < 2) == (way == 0) else 7

                @pl.when(it <= last)
                def _():
                    z_copy(way, k, it).wait_send()

            last = 8 - way

            @pl.when(it <= last)
            def _():
                code_copy(way, it, it).wait_send()

            core_copy(way, it, z, c).wait_send()
            for hop in range(3):
                x_copy(hop, way, it, sums.at[0, way, it]).wait_send()
        return carry

    lax.fori_loop(1, 9, drain, 0)

    def sent_all(dz, dy):
        at_z, at_y = lax.rem(z + dz, 16), lax.rem(y + dy, 4)
        row_copy(dz, dy, at_z, at_y).wait_send()
        end_copy(dz, dy, at_z, at_y).wait_send()

    others(sent_all)
    swap.wait_send()
    for dx in range(1, 4):
        for t in range(3):
            mix_copies(dx, t).wait_send()


def ensemble(tile, code, own, low, high, weights, prior, q_head, l_head):
    rows, chunk = tile.shape
    entries = q_head.shape[0] + l_head.shape[0]
    vmem = pl.BlockSpec(memory_space=pltpu.VMEM)
    dma = pltpu.SemaphoreType.DMA
    bf16, f32 = jnp.bfloat16, jnp.float32
    return pl.pallas_call(
        ensemble_kernel,
        out_shape=(
            jax.ShapeDtypeStruct((256, 2 * BLOCK), f32),
            jax.ShapeDtypeStruct((4, 8, BLOCK), f32),
        ),
        in_specs=[*[vmem] * 7, *[pl.BlockSpec(memory_space=pltpu.HBM)] * 2],
        out_specs=(vmem, vmem),
        scratch_shapes=[
            pltpu.VMEM((16, 2, 4, rows, chunk), bf16),
            pltpu.VMEM((16, rows, BLOCK), bf16),
            pltpu.VMEM(q_head.shape, bf16),
            pltpu.VMEM(l_head.shape, bf16),
            pltpu.VMEM((B_DEV, 4 * rows, BLOCK), f32),
            pltpu.VMEM((9, 2, 4, 8, entries), f32),
            pltpu.VMEM((3, 2, 9, 8, entries), f32),
            pltpu.VMEM((16 * 64, BLOCK), f32),
            pltpu.VMEM((16, 4, 16, BLOCK), bf16),
            pltpu.VMEM((2, 16, 4, 16, BLOCK), bf16),
            pltpu.VMEM((2048, BLOCK), f32),
            pltpu.VMEM((2, 4, 64, BLOCK), bf16),
            pltpu.VMEM((2, 4, 64, BLOCK), bf16),
            pltpu.VMEM((8, BLOCK), f32),
            pltpu.VMEM((4, 8, BLOCK), f32),
            pltpu.VMEM((16, 4, 8, BLOCK), bf16),
            pltpu.VMEM((16, 4, 8, BLOCK), bf16),
            pltpu.VMEM((B_DEV * BLOCK, BLOCK), f32),
            dma((2,)),
            *[dma((3,))] * 2,
            *[dma((2, 4, 9))] * 2,
            *[dma((2, 9))] * 2,
            *[dma((2, 9))] * 2,
            *[dma((3, 2, 9))] * 2,
            *[dma((16, 4))] * 2,
            *[dma(())] * 2,
            *[dma((3, 4))] * 2,
            *[dma((16, 4))] * 2,
        ],
        compiler_params=pltpu.CompilerParams(
            collective_id=0, has_side_effects=True, vmem_limit_bytes=56 * 1024 * 1024
        ),
        cost_estimate=pl.CostEstimate(flops=3 * 10**10, bytes_accessed=10**7, transcendentals=0),
    )(tile, code, own, low, high, weights, prior, q_head, l_head)


def by_source(codes, per_device):
    return codes.reshape(-1, 2, per_device).transpose(2, 1, 0).reshape(per_device, -1)


def local(
    qwen_hidden,
    qwen_next_hidden,
    llama_hidden,
    llama_next_hidden,
    qwen_head,
    llama_head,
    align_weights,
    qwen_links,
    llama_links,
    union_order,
    chosen,
    model_weight,
):
    core = lax.axis_index("vocab_2")
    owner = lax.axis_index(VOCAB)
    hidden_cat = jnp.concatenate(
        [qwen_hidden, qwen_next_hidden, llama_hidden, llama_next_hidden], axis=1
    )
    tile, code = column_tile(hidden_cat, chosen)
    q_low, q_high = link_codes(qwen_links, union_order, qwen_links.shape[0] // 2)
    l_low, l_high = link_codes(llama_links, union_order, llama_links.shape[0] // 2)
    low, high = (
        jnp.concatenate([by_source(q, QB_DEV), by_source(l, LB_DEV)])
        for q, l in ((q_low, l_low), (q_high, l_high))
    )
    q_own = own_codes(qwen_links, owner * QB_DEV, QB_DEV)
    l_own = own_codes(llama_links, owner * LB_DEV, LB_DEV)
    own = jnp.concatenate([jnp.pad(jnp.concatenate(pair), (0, 16 - B_DEV)) for pair in zip(q_own, l_own)])
    own = jnp.broadcast_to(own.astype(jnp.float32)[:, None], (32, BLOCK))
    prior = model_weight / (model_weight[0] + model_weight[1])
    prior = jnp.broadcast_to(prior[:, None], (2, BLOCK))
    next_logprob, logliks = ensemble(
        tile, code, own, low, high, align_weights, prior, qwen_head, llama_head
    )
    return next_logprob, lax.dynamic_slice(logliks[:, 0, 0], (2 * core,), (2,))


def solution(mesh):
    torus = Mesh(
        mesh.devices.reshape(16, 4, 2, mesh.shape["width"]),
        ("vocab_0", "vocab_1", "vocab_2", "width"),
    )
    return jax.shard_map(
        local,
        mesh=torus,
        in_specs=(*[P(VOCAB, "width")] * 6, P(), P(), P(), P(), P(VOCAB), P()),
        out_specs=(P(None, (*VOCAB, "width")), P(VOCAB)),
        check_vma=False,
    )
```

time: 272 us -> 124 us (0.46)
  waiting for transfers between devices: 137 us -> 0.01 us
  Pallas kernels: 4.13 us -> 92.5 us
  blocking collectives: 36.7 us -> 0 us
  between operations: 19.9 us -> 2.07 us
  starting transfers between devices: 27.6 us -> 10.1 us
  other arithmetic: 20.2 us -> 8.86 us
  local copies, waits for them, and re-layouts: 18 us -> 10.2 us
  matrix products: 6.99 us -> 0 us
    all_gather x2 -> x0, waiting for transfers between devices: 95.1 us -> none  [the longest x1 66.4 us: gathered_tiles(): tiles = lax.all_gather(tiles, 'vocab_0')]
    pallas_call x1, Pallas kernels: 4.13 us -> 92.5 us  [ensemble(): pl.pallas_call(ensemble_kernel, out_shape=(jax.ShapeDtypeStruct((256, 2 *...]
    all_to_all x3 -> x1, waiting for transfers between devices: 42.3 us -> 0.01 us  [column_tile(): lax.all_to_all(jnp.concatenate([parts, codes], axis=2), GROUP, 0, 0, tile...]
    all_to_all x3 -> x1, starting transfers between devices: 27.6 us -> 10.1 us  [column_tile(): lax.all_to_all(jnp.concatenate([parts, codes], axis=2), GROUP, 0, 0, tile...]
    all_gather x2 -> x0, blocking collectives: 15.3 us -> none  [the longest x1 9.88 us: gathered_tiles(): tiles = lax.all_gather(tile, 'vocab_1')]
    all_to_all x1 -> x0, blocking collectives: 13.9 us -> none  [gathered_tiles(): lax.all_to_all(jnp.concatenate([parts, codes], axis=2), GROUP, 0, 0, tile...]
    unnamed x1 -> x0, blocking collectives: 7.38 us -> none
    dot_general x9 -> x0, matrix products: 6.99 us -> none  [the longest x8 6.78 us: partial_logits(): lax.dot_general(rows, head[:, half * chunk:(half + 1) * chunk], (((1,), (...]
  transfers between devices with their start and end apart: 5 -> 1, of which waited for: 5 -> 0; matrix products, arithmetic and copies ran while one was open for 6% -> 9% of each run, Pallas kernels for 0% -> 0%
where the time goes in v2:
time: 124 us
  Pallas kernels  92.5 us (75%)
  local copies, waits for them, and re-layouts  10.2 us (8%)
  starting transfers between devices  10.1 us (8%)
  other arithmetic  8.86 us (7%)
  between operations  2.07 us (2%)
    pallas_call x1, Pallas kernels, ensemble(): pl.pallas_call(ensemble_kernel, out_shape=(jax.ShapeDtypeStruct((256, 2 *...  92.5 us
    all_to_all x1, starting transfers between devices, column_tile(): lax.all_to_all(jnp.concatenate([parts, codes], axis=2), GROUP, 0, 0, tile...  10.1 us
    reduce_sum x2, other arithmetic, positions_of(): jnp.sum(jnp.where(union_order[None, :] == blocks[:, None], places[None, :...  2.88 us
  transfers between devices with their start and end apart: 1, of which 0 were waited for; matrix products, arithmetic and copies ran while one was open for 9% of the time, Pallas kernels for 0%

profile of v2, /device:TPU:1, one launch (start us, length us, event | category | flops | bytes accessed | tf_op | source)
XLA Modules:
  0.0 123.7 jit_solution(10057227378601204474)
XLA Ops:
  0.6 0.7 convert_bitcast_fusion
  1.5 0.8 pad_maximum_fusion.1
  2.2 0.7 pad_maximum_fusion
  2.9 10.1 %all-to-all-start = ((bf16[8,2,1152]{2,1,0:T(2,128)(2,1)}), bf16[8,2,1152]{2,1,0:T(2,128)(2,1)S(1)}, u32[]{:S(2)}, u32[]{:S(2)}) async-start(bf16[8,2,1152]{2,1,0:T(2,128)(2,1)} %pad_maximum_fusion), calls=%async_computation | async-start | bytes 73728 | tf_op jit(solution)/shard_map/all_to_all | solution.py:55
  13.0 1.3 %fusion.10 = (f32[1]{0:T(128)}, f32[1]{0:T(128)}) fusion(f32[2]{0:T(128)} %param.23), kind=kLoop, calls=%fused_computation.52 | loop fusion | bytes 16 | tf_op jit(solution)/shard_map/slice | solution.py:606
  15.7 0.7 broadcast_divide_fusion
  16.3 0.8 fusion.9
  17.2 0.9 slice_reduce_fusion.2
  18.1 1.4 %select_reduce_fusion.1 = s32[1024]{0:T(1024)S(1)} fusion(s32[1024]{0:T(1024)} %param.21, s32[1024]{0:T(1024)S(1)} %bitcast.22), kind=kLoop, calls=%fused_computation.1 | loop fusion | flops 3144704 | bytes 12288 | tf_op jit(solution)/shard_map/reduce_sum | solution.py:26
  19.4 1.5 %select_reduce_fusion = s32[1280]{0:T(1024)S(1)} fusion(s32[1024]{0:T(1024)} %param.21, s32[1280]{0:T(1024)S(1)} %get-tuple-element.8), kind=kLoop, calls=%fused_computation | loop fusion | flops 3930880 | bytes 14336 | tf_op jit(solution)/shard_map/reduce_sum | solution.py:26
  21.0 1.2 select_reduce_fusion.2
  22.2 0.2 reshape.106
  22.6 0.8 select_reduce_fusion.4
  23.7 0.3 reshape.102
  24.7 0.2 fusion
  25.0 0.6 pad_add_fusion
  25.7 0.6 slice.51.code_ref
  26.3 0.6 slice.50.tile_ref
  26.9 0.7 broadcast_in_dim.148.prior_ref
  27.6 0.7 broadcast_in_dim.137.own_ref
  28.2 92.5 %shard_map.131 = (f32[256,256]{1,0:T(8,128)}, f32[4,8,128]{2,1,0:T(8,128)}) custom-call(bf16[16,1024]{1,0:T(8,128)(2,1)} %slice.50.tile_ref, bf16[16,128]{1,0:T(8,128)(2,1)} %slice.51.code_ref, f32[32,128]{1,0:T(8,128)} %broadcast_in_dim.137.own_ref, s32[9,128]{1,0:T(8,128)} %get-tuple-element.31.low_ref, s32[9,128]{1,0:T(8,128)} %get-tuple-element.32.high_ref, ...), custom_call_target="tpu_custom_call" | custom-call | flops 30000001024 | bytes 10000000 | tf_op jit(solution)/shard_map/pallas_call | solution.py:527
  120.7 0.7 slice.49
  121.4 0.6 dynamic-slice_reduce_fusion
  122.0 1.7 %copy.30 = f32[256,256]{1,0:T(8,128)} copy(f32[256,256]{1,0:T(8,128)} %get-tuple-element.35) | data formatting | bytes 524288
  (24 shorter events, 1.5 us)
Async XLA Ops:
  2.9 22.8 %all-to-all-start = ((bf16[8,2,1152]{2,1,0:T(2,128)(2,1)}), bf16[8,2,1152]{2,1,0:T(2,128)(2,1)S(1)}, u32[]{:S(2)}, u32[]{:S(2)}) async-start(bf16[8,2,1152]{2,1,0:T(2,128)(2,1)} %pad_maximum_fusion), calls=%async_computation | async-start | bytes 73728 | tf_op jit(solution)/shard_map/all_to_all | solution.py:55
